TPU v7x, 32 devices: a whole 2x2x4 slice. The times are simulated.
32 devices in a mesh: env: 32 (over z, y, x, core).
Axes of the slice: x: 2, y: 2, z: 4, core: 2. Of those that a mesh axis runs over, the one named last changes fastest.
Arguments:
- observations: bfloat16 [16, 512, 96], P(None, 'env'), may hold values from -6 to 6
- physics_params: bfloat16 [512, 32], P('env'), may hold values from -4 to 4
- actions: int32 [16, 512, 20], P(None, 'env'), may hold values from 0 to 10
- reset_step: int32 [512], P('env'), may hold values from 0 to 16
- hidden_start: bfloat16 [512, 1024], P('env'), may hold values from -0.8984375 to 0.8984375
- cell_start: float32 [512, 1024], P('env'), may hold values from -4 to 4
- old_logp: float32 [16, 512], P(None, 'env'), may hold values from -50.5 to -47.5
- advantages: float32 [16, 512], P(None, 'env'), may hold values from 3 to 7
- returns: float32 [16, 512], P(None, 'env'), may hold values from -5 to 5
- lstm_weight: bfloat16 [1152, 4096], replicated, may hold values from -0.1875 to 0.1875
- lstm_bias: float32 [4096], replicated, may hold values from -4 to 4
- head_weight: bfloat16 [1024, 221], replicated, may hold values from -0.1875 to 0.1875
Outputs:
- lstm_step: float32 [1152, 4096], P('env')
- bias_step: float32 [4096], P('env')
- head_step: float32 [1024, 221], P('env')
- kl_mean: float32 [], replicated
All inputs are finite; a program needn't handle non-finite values.
Results may differ from a plain program's by a relative error of at most 0.0073.
Values sent between devices are 32-bit elements; how exact they have to be, the bound alone decides.
A program may use at most 128 MiB of HBM per device.

v0:
```python
import jax
import jax.numpy as jnp
from jax import lax
from jax.sharding import PartitionSpec as P

kl_coef = 0.5
value_coef = 0.5
spread_floor = 0.25


def local_terms(
    observations,
    physics_params,
    actions,
    reset_step,
    hidden_start,
    cell_start,
    old_logp,
    norm_adv,
    returns,
    lstm_weight,
    lstm_bias,
    head_weight,
):
    step_count, env_count = (observations.shape[0], observations.shape[1])
    hidden = hidden_start.shape[1]
    width_in = lstm_weight.shape[0] - hidden
    act_count = actions.shape[2]
    bin_count = (head_weight.shape[1] - 1) // act_count
    phys_tiled = jnp.broadcast_to(
        physics_params[None], (step_count, env_count, physics_params.shape[1])
    )
    inputs = jnp.concatenate([observations, phys_tiled], axis=2).reshape(
        step_count * env_count, width_in
    )
    w_rec = lstm_weight[width_in:]
    projected = (
        jnp.dot(inputs, lstm_weight[:width_in], preferred_element_type=jnp.float32) + lstm_bias
    )
    projected = projected.reshape(step_count, env_count, 4 * hidden)
    columns = lax.broadcasted_iota(jnp.int32, (1, 4 * hidden), 1)
    is_cand = (columns >= 2 * hidden) & (columns < 3 * hidden)
    step_ids = jnp.arange(step_count, dtype=jnp.int32)

    def advance(state_pair, inputs_now):
        h_prev, c_prev = state_pair
        proj_now, step_index = inputs_now
        keep_mask = (reset_step != step_index)[:, None]
        h_kept = jnp.where(keep_mask, h_prev, jnp.zeros_like(h_prev))
        c_kept = jnp.where(keep_mask, c_prev, jnp.zeros_like(c_prev))
        pre_act = proj_now + jnp.dot(h_kept, w_rec, preferred_element_type=jnp.float32)
        activated = jnp.where(is_cand, jnp.tanh(pre_act), jax.nn.sigmoid(pre_act))
        gate_i = activated[:, :hidden]
        gate_f = activated[:, hidden : 2 * hidden]
        cand_gate = activated[:, 2 * hidden : 3 * hidden]
        gate_o = activated[:, 3 * hidden :]
        c_new = gate_f * c_kept + gate_i * cand_gate
        tanh_c = jnp.tanh(c_new)
        h_new = (gate_o * tanh_c).astype(jnp.bfloat16)
        return ((h_new, c_new), (h_kept, c_kept, activated, tanh_c, h_new))

    final_state, saved = lax.scan(advance, (hidden_start, cell_start), (projected, step_ids))
    h_kept_all, c_kept_all, activated_all, tanh_all, hseq = saved
    h_flat = hseq.reshape(step_count * env_count, hidden)
    logits = jnp.dot(h_flat, head_weight, preferred_element_type=jnp.float32)
    policy = logits[:, : act_count * bin_count].reshape(-1, act_count, bin_count)
    value_pred = logits[:, act_count * bin_count]
    exp_policy = jnp.exp(policy)
    sum_exp = jnp.sum(exp_policy, axis=2, keepdims=True)
    soft_probs = exp_policy / sum_exp
    log_probs = policy - jnp.log(sum_exp)
    levels = lax.broadcasted_iota(jnp.int32, (1, 1, bin_count), 2)
    onehot = (actions.reshape(-1, act_count)[:, :, None] == levels).astype(jnp.float32)
    token_logp = jnp.sum(onehot * log_probs, axis=(1, 2))
    log_ratio = token_logp - old_logp.reshape(-1)
    prob_ratio = jnp.exp(log_ratio)
    kl_part = jnp.sum(prob_ratio - 1.0 - log_ratio)
    grad_logp = kl_coef * (prob_ratio - 1.0) - norm_adv.reshape(-1) * prob_ratio
    grad_policy = grad_logp[:, None, None] * (onehot - soft_probs)
    grad_value = value_coef * (value_pred - returns.reshape(-1))
    grad_logits = jnp.concatenate(
        [grad_policy.reshape(-1, act_count * bin_count), grad_value[:, None]], axis=1
    ).astype(jnp.bfloat16)
    head_grad = lax.dot_general(
        h_flat, grad_logits, (((0,), (0,)), ((), ())), preferred_element_type=jnp.float32
    )
    from_head = lax.dot_general(
        grad_logits, head_weight, (((1,), (1,)), ((), ())), preferred_element_type=jnp.float32
    )
    from_head = from_head.reshape(step_count, env_count, hidden)

    def retreat(state_pair, inputs_now):
        grad_h_next, grad_c_next = state_pair
        c_kept, activated, tanh_c, head_part, step_index = inputs_now
        keep_mask = (reset_step != step_index)[:, None]
        gate_i = activated[:, :hidden]
        gate_f = activated[:, hidden : 2 * hidden]
        cand_gate = activated[:, 2 * hidden : 3 * hidden]
        gate_o = activated[:, 3 * hidden :]
        grad_h = head_part + grad_h_next
        grad_c = grad_c_next + grad_h * gate_o * (1.0 - tanh_c * tanh_c)
        upstream = jnp.concatenate(
            [grad_c * cand_gate, grad_c * c_kept, grad_c * gate_i, grad_h * tanh_c], axis=1
        )
        act_slope = jnp.where(is_cand, 1.0 - activated * activated, activated * (1.0 - activated))
        grad_gates = (upstream * act_slope).astype(jnp.bfloat16)
        grad_h_prev = lax.dot_general(
            grad_gates, w_rec, (((1,), (1,)), ((), ())), preferred_element_type=jnp.float32
        )
        grad_h_prev = jnp.where(keep_mask, grad_h_prev, jnp.zeros_like(grad_h_prev))
        grad_c_prev = jnp.where(keep_mask, grad_c * gate_f, jnp.zeros_like(grad_c))
        return ((grad_h_prev, grad_c_prev), grad_gates)

    zero_state = jnp.zeros((env_count, hidden), jnp.float32)
    final_grads, grad_gates = lax.scan(
        retreat,
        (zero_state, zero_state),
        (c_kept_all, activated_all, tanh_all, from_head, step_ids),
        reverse=True,
    )
    operand = jnp.concatenate([inputs, h_kept_all.reshape(step_count * env_count, hidden)], axis=1)
    return (operand, grad_gates.reshape(step_count * env_count, 4 * hidden), head_grad, kl_part)


def shards(
    observations,
    physics_params,
    actions,
    reset_step,
    hidden_start,
    cell_start,
    old_logp,
    advantages,
    returns,
    lstm_weight,
    lstm_bias,
    head_weight,
):
    token_total = advantages.size * lax.axis_size("env")
    local_sum = jnp.sum(advantages)
    adv_sum, adv_squares = lax.psum((local_sum, jnp.sum(advantages * advantages)), "env")
    adv_mean = adv_sum / token_total
    spread = adv_squares / token_total - adv_mean * adv_mean
    norm_adv = (advantages - adv_mean) / jnp.sqrt(spread + spread_floor)
    operand, grad_gates, head_grad, kl_part = local_terms(
        observations,
        physics_params,
        actions,
        reset_step,
        hidden_start,
        cell_start,
        old_logp,
        norm_adv,
        returns,
        lstm_weight,
        lstm_bias,
        head_weight,
    )
    kl_total = lax.psum(kl_part, "env")
    bias_grad = jnp.sum(grad_gates.astype(jnp.float32), axis=0)
    lstm_grad = lax.dot_general(
        operand, grad_gates, (((0,), (0,)), ((), ())), preferred_element_type=jnp.float32
    )
    lstm_part, bias_part, head_part = (
        lax.psum_scatter(lstm_grad, "env", scatter_dimension=0, tiled=True),
        lax.psum_scatter(bias_grad, "env", scatter_dimension=0, tiled=True),
        lax.psum_scatter(head_grad, "env", scatter_dimension=0, tiled=True),
    )
    local_squares = (
        jnp.sum(lstm_part * lstm_part)
        + jnp.sum(bias_part * bias_part)
        + jnp.sum(head_part * head_part)
    )
    grad_sq = lax.psum(local_squares, "env")
    param_total = lstm_weight.size + lstm_bias.size + head_weight.size
    scale = 1.0 / jnp.sqrt(grad_sq / param_total + 1.0)
    return (lstm_part * scale, bias_part * scale, head_part * scale, kl_total / token_total)


def solution(mesh):
    in_specs = (
        P(None, "env", None),
        P("env", None),
        P(None, "env", None),
        P("env"),
        P("env", None),
        P("env", None),
        P(None, "env"),
        P(None, "env"),
        P(None, "env"),
        P(),
        P(),
        P(),
    )
    out_specs = (P("env", None), P("env"), P("env", None), P())
    return jax.shard_map(shards, mesh=mesh, in_specs=in_specs, out_specs=out_specs, check_vma=False)
```

profile of v0, /device:TPU:0, one launch (start us, length us, event | category | flops | bytes accessed | tf_op | source)
XLA Modules:
  0.0 759.3 jit_solution(10687949003266583225)
XLA Ops:
  7.3 7.8 %slice.61 = bf16[1024,4096]{1,0:T(8,128)(2,1)} slice(bf16[1152,4096]{1,0:T(8,128)(2,1)} %param.25), slice={[128:1152], [0:4096]} | slice | bytes 16777216 | tf_op jit(solution)/shard_map/slice | solution.py:36
  19.2 119.4 %while.43 = (s32[]{:T(128)}, bf16[16,1024]{1,0:T(8,128)(2,1)S(1)}, f32[16,1024]{1,0:T(8,128)S(1)}, bf16[16,16,1024]{2,1,0:T(8,128)(2,1)S(1)}, f32[16,16,1024]{2,...) while((s32[]{:T(128)}, bf16[16,1024]{1,0:T(8,128)(2,1)S(1)}, ...), condition=%wide.region_1.0_spmd.clone, body=%wide.region_0.0_spmd.clone.sunk | while | flops 134705168 | bytes 10135297 | solution.py:62
  27.9 5.4 bitcast_dynamic-update-slice_fusion.8
  35.4 5.4 bitcast_dynamic-update-slice_fusion.8
  87.6 5.4 bitcast_dynamic-update-slice_fusion.8
  95.1 5.4 bitcast_dynamic-update-slice_fusion.8
  117.5 5.4 bitcast_dynamic-update-slice_fusion.8
  132.4 5.4 bitcast_dynamic-update-slice_fusion.8
  142.0 42.2 %all-reduce.4 = (f32[]{:T(128)}, f32[]{:T(128)}) all-reduce(f32[]{:T(128)} %get-tuple-element.413, f32[]{:T(128)} %get-tuple-element.412), channel_id=1, replica_groups=mesh['env'=32] {'env'}, use_global_device_ids=true, to_apply=%region_7.8 | all-reduce | flops 2 | bytes 16 | tf_op jit(solution)/shard_map/psum | solution.py:141
  190.9 193.6 %while.44 = (s32[]{:T(128)}, f32[16,1024]{1,0:T(8,128)S(1)}, f32[16,1024]{1,0:T(8,128)S(1)}, bf16[16,16,4096]{2,1,0:T(8,128)(2,1)S(1)}, s32[16]{0:T(128)}, /*ind...) while((s32[]{:T(128)}, f32[16,1024]{1,0:T(8,128)S(1)}, ...), condition=%wide.region_9.10_spmd.clone.clone, body=%wide.region_8.9_spmd.clone.clone.sunk | while | flops 135786512 | bytes 11219243 | solution.py:115
  197.3 5.6 convolution_select_fusion.2
  209.4 5.7 convolution_select_fusion.2
  221.5 5.6 convolution_select_fusion.2
  233.6 5.7 convolution_select_fusion.2
  245.7 5.6 convolution_select_fusion.2
  257.8 5.7 convolution_select_fusion.2
  269.9 5.6 convolution_select_fusion.2
  282.0 5.7 convolution_select_fusion.2
  294.1 5.7 convolution_select_fusion.2
  306.2 5.7 convolution_select_fusion.2
  318.3 5.7 convolution_select_fusion.2
  330.4 5.6 convolution_select_fusion.2
  342.5 5.6 convolution_select_fusion.2
  354.6 5.6 convolution_select_fusion.2
  366.7 5.6 convolution_select_fusion.2
  378.8 5.6 convolution_select_fusion.2
  384.4 7.8 %fusion.26 = f32[1152,4096]{1,0:T(8,128)} fusion(bf16[256,4096]{1,0:T(8,128)(2,1)S(1)} %bitcast.88, bf16[256,1024]{1,0:T(8,128)(2,1)S(1)} %bitcast.99, bf16[256,128]{1,0:T(8,128)(2,1)S(1)} %bitcast.98), kind=kOutput, calls=%fused_computation.53 | convolution fusion | flops 2417098752 | bytes 21561344 | tf_op jit(solution)/shard_map/dot_general | solution.py:161
  392.2 216.2 %fusion.4 = f32[40,4096]{1,0:T(8,128)S(1)} fusion(f32[1152,4096]{1,0:T(8,128)} %fusion.26), kind=kCustom, calls=%all-reduce-scatter | all-reduce-scatter fusion | flops 5242881 | bytes 19529728
  608.5 15.4 %collective-permute-start = (f32[40,4096]{1,0:T(8,128)S(1)}, f32[40,4096]{1,0:T(8,128)}, u32[]{:S(2)}, u32[]{:S(2)}) collective-permute-start(f32[40,4096]{1,0:T(8,128)S(1)} %fusion.4), channel_id=1, source_target_pairs={{0,1},{1,2},{2,3},{3,4},{4,5},{5,6},{6,7},{7,8},{8,9},{9,10},{10,1... | collective-permute-start | bytes 1966088
  633.2 58.7 %all-reduce.1 = f32[4096]{0:T(1024)S(1)} all-reduce(f32[4096]{0:T(1024)S(1)} %convert_reduce_fusion), channel_id=3, replica_groups=mesh['env'=32] {'env'}, use_global_device_ids=true, to_apply=%region_13.14.clone | all-reduce | flops 4096 | bytes 32768
  693.2 8.4 %concatenate.51 = f32[164,4096]{1,0:T(8,128)S(1)} concatenate(f32[4,4096]{1,0:T(4,128)S(1)} %collective-permute-done.3, f32[40,4096]{1,0:T(8,128)} %collective-permute-done.2, f32[40,4096]{1,0:T(8,128)} %collective-permute-done.1, f32[40,4096]{1,0:T(8,128)} %collective-permute-done, f32[40,4096]{1,0:T(8,128)} %copy-done.3), dimensions={0} | concatenate | bytes 5373952
  705.8 41.3 %all-reduce.3 = (f32[]{:T(128)}, f32[]{:T(128)}) all-reduce(f32[]{:T(128)S(6)} %add.90, f32[]{:T(128)} %subtract_reduce_fusion), channel_id=1, replica_groups=mesh['env'=32] {'env'}, use_global_device_ids=true, to_apply=%region_17.18 | all-reduce | flops 2 | bytes 16 | tf_op jit(solution)/shard_map/psum | solution.py:174
  (298 shorter events, 216.9 us)
Async XLA Ops:
  7.2 131.5 %copy-start = (bf16[1024,221]{0,1:T(8,128)(2,1)S(1)}, bf16[1024,221]{0,1:T(8,128)(2,1)}, u32[]{:S(2)}) copy-start(bf16[1024,221]{0,1:T(8,128)(2,1)} %param.27) | copy-start | bytes 1357828
  7.2 696.6 %reduce-scatter.4.cloned.1.call-start = ((), (), s32[]{:S(2)}) async-start(), calls=%async_computation.1 | async-start | bytes 1081344 | tf_op jit(solution)/shard_map/reduce_scatter | solution.py:167
  7.3 7.8 %copy-start.10 = (bf16[16,32]{1,0:T(8,128)(2,1)S(1)}, bf16[16,32]{1,0:T(8,128)(2,1)}, u32[]{:S(2)}) copy-start(bf16[16,32]{1,0:T(8,128)(2,1)} %param.17) | copy-start | bytes 3076
  7.3 7.8 %copy-start.5 = (bf16[16,16,96]{2,1,0:T(8,128)(2,1)S(1)}, bf16[16,16,96]{2,1,0:T(8,128)(2,1)}, u32[]{:S(2)}) copy-start(bf16[16,16,96]{2,1,0:T(8,128)(2,1)} %param.16) | copy-start | bytes 147460
  7.3 7.9 %copy-start.8 = (f32[4096]{0:T(1024)S(1)}, f32[4096]{0:T(1024)}, u32[]{:S(2)}) copy-start(f32[4096]{0:T(1024)} %param.26) | copy-start | bytes 49156
  15.1 4.1 copy-start.1
  15.1 4.1 copy-start.2
  15.1 4.1 copy-start.11
  19.1 121.9 %copy-start.4 = (s32[16,16,20]{2,1,0:T(8,128)S(1)}, s32[16,16,20]{2,1,0:T(8,128)}, u32[]{:S(2)}) copy-start(s32[16,16,20]{2,1,0:T(8,128)} %param.18) | copy-start | bytes 61444
  138.6 2.7 copy-start.6
  138.6 48.3 %copy-start.7 = (f32[16,16]{1,0:T(8,128)S(1)}, f32[16,16]{1,0:T(8,128)}, u32[]{:S(2)}) copy-start(f32[16,16]{1,0:T(8,128)} %param.22) | copy-start | bytes 3076
  138.6 48.4 %copy-start.9 = (f32[16,16]{1,0:T(8,128)S(1)}, f32[16,16]{1,0:T(8,128)}, u32[]{:S(2)}) copy-start(f32[16,16]{1,0:T(8,128)} %param.24) | copy-start | bytes 3076
  608.4 84.8 %copy-start.3 = (f32[40,4096]{1,0:T(8,128)}, f32[40,4096]{1,0:T(8,128)S(1)}, u32[]{:S(2)}) copy-start(f32[40,4096]{1,0:T(8,128)S(1)} %fusion.4) | copy-start | bytes 1966084
  608.5 84.7 %collective-permute-start = (f32[40,4096]{1,0:T(8,128)S(1)}, f32[40,4096]{1,0:T(8,128)}, u32[]{:S(2)}, u32[]{:S(2)}) collective-permute-start(f32[40,4096]{1,0:T(8,128)S(1)} %fusion.4), channel_id=1, source_target_pairs={{0,1},{1,2},{2,3},{3,4},{4,5},{5,6},{6,7},{7,8},{8,9},{9,10},{10,1... | collective-permute-start | bytes 1966088
  623.8 69.4 %collective-permute-start.1 = (f32[40,4096]{1,0:T(8,128)S(1)}, f32[40,4096]{1,0:T(8,128)}, u32[]{:S(2)}, u32[]{:S(2)}) collective-permute-start(f32[40,4096]{1,0:T(8,128)S(1)} %fusion.4), channel_id=1, source_target_pairs={{0,2},{1,3},{2,4},{3,5},{4,6},{5,7},{6,8},{7,9},{8,10},{9,11},{10,... | collective-permute-start | bytes 1966088
  628.1 65.1 %collective-permute-start.2 = (f32[40,4096]{1,0:T(8,128)S(1)}, f32[40,4096]{1,0:T(8,128)}, u32[]{:S(2)}, u32[]{:S(2)}) collective-permute-start(f32[40,4096]{1,0:T(8,128)S(1)} %fusion.4), channel_id=1, source_target_pairs={{0,3},{1,4},{2,5},{3,6},{4,7},{5,8},{6,9},{7,10},{8,11},{9,12},{10... | collective-permute-start | bytes 1966088
  631.5 61.7 %collective-permute-start.3 = (f32[4,4096]{1,0:T(4,128)S(1)}, f32[4,4096]{1,0:T(4,128)S(1)}, u32[]{:S(2)}, u32[]{:S(2)}) collective-permute-start(f32[4,4096]{1,0:T(4,128)S(1)} %slice.86), channel_id=1, source_target_pairs={{0,4},{1,5},{2,6},{3,7},{4,8},{5,9},{6,10},{7,11},{8,12},{9,13},{1... | collective-permute-start | bytes 196616
Sparse Core Ops, SparseCore 0:
  188.8 136.7 reduce-scatter.3
where the time goes:
time: 764 us; the launch traced here: 759 us
  blocking collectives  358 us (47%)
  matrix products  191 us (25%)
  other arithmetic  101 us (13%)
  local copies, waits for them, and re-layouts  62.8 us (8%)
  starting transfers between devices  24.3 us (3%)
  between operations  21.5 us (3%)
    unnamed x2, blocking collectives  275 us
    dot_general x16, matrix products, retreat(): lax.dot_general(grad_gates, w_rec, (((1,), (1,)), ((), ())), preferred_el...  90.5 us
    dot_general x16, matrix products, advance(): jnp.dot(h_kept, w_rec, preferred_element_type=jnp.float32)  85.8 us
    psum x1, blocking collectives, shards(): lax.psum((local_sum, jnp.sum(advantages * advantages)), 'env')  42.2 us
    psum x1, blocking collectives, shards(): grad_sq = lax.psum(local_squares, 'env')  41.3 us
    dynamic_slice x32, local copies, waits for them, and re-layouts, local_terms(): lax.scan(advance, (hidden_start, cell_start), (projected, step_ids))  29.2 us
    unnamed x4, starting transfers between devices  24.3 us
    ne x16, other arithmetic, retreat(): keep_mask = (reset_step != step_index)[:, None]  20.9 us
  transfers between devices with their start and end apart: 5, of which 0 were waited for; matrix products, arithmetic and copies ran while one was open for 57% of the time, Pallas kernels for 0%

commit v1 on v0

v1 whole, which is shorter than its diff:
```python
import functools
import math

import jax
import jax.numpy as jnp
from jax import lax
from jax.experimental import pallas as pl
from jax.experimental.pallas import tpu as pltpu
from jax.sharding import PartitionSpec as P

kl_coef = 0.5
value_coef = 0.5
spread_floor = 0.25
f32 = jnp.float32
bf16 = jnp.bfloat16
MESH = pl.DeviceIdType.MESH
NT = (((1,), (1,)), ((), ()))
TN = (((0,), (0,)), ((), ()))


def sigmoid(x):
    return 0.5 * jnp.tanh(0.5 * x) + 0.5


def kernel(
    sizes,
    x_ref,
    act_ref,
    reset_ref,
    h0_ref,
    c0_ref,
    aux_ref,
    w_ref,
    bias_ref,
    hw_ref,
    same_ref,
    spread_ref,
    level_ref,
    dw_ref,
    db_ref,
    dh_ref,
    kl_ref,
    gates,
    ck_all,
    tc_all,
    hseq,
    hk_b,
    h_now,
    c_now,
    gg_b,
    head_part,
    all_h,
    all_g,
    all_x,
    hs_sem,
    hr_sem,
    fs_sem,
    fr_sem,
    gs_sem,
    gr_sem,
    xs_sem,
    xr_sem,
):
    steps, envs, hidden, width_in, group, policy_cols = sizes
    chips = group // 2
    me = lax.axis_index("env")
    mine = lax.rem(me, group)
    base = me - mine
    core = lax.rem(mine, 2)
    chip = mine // 2
    partner = chip * 2 + (1 - core)
    part = 4 * hidden // group
    chunk = 256

    def other(k):
        return lax.rem(mine + k, group)

    def same_core(k):
        return lax.rem(chip + k, chips) * 2 + core

    barrier = pltpu.get_barrier_semaphore()
    for k in range(1, group):
        pl.semaphore_signal(barrier, inc=1, device_id=(base + other(k),), device_id_type=MESH)
    pl.semaphore_wait(barrier, group - 1)

    def x_copy(k):
        return pltpu.make_async_remote_copy(
            src_ref=x_ref,
            dst_ref=all_x.at[mine],
            send_sem=xs_sem.at[k - 1],
            recv_sem=xr_sem.at[k - 1],
            device_id=(base + other(k),),
            device_id_type=MESH,
        )

    def h_copy(k, rows):
        return pltpu.make_async_remote_copy(
            src_ref=all_h.at[mine, rows],
            dst_ref=all_h.at[mine, rows],
            send_sem=hs_sem.at[k - 1],
            recv_sem=hr_sem.at[k - 1],
            device_id=(base + same_core(k),),
            device_id_type=MESH,
        )

    def forward_copy(k):
        block = same_core(k)
        return pltpu.make_async_remote_copy(
            src_ref=all_h.at[block],
            dst_ref=all_h.at[block],
            send_sem=fs_sem.at[k],
            recv_sem=fr_sem.at[k],
            device_id=(base + partner,),
            device_id_type=MESH,
        )

    def g_copy(k, rows):
        target = other(k)
        cols = pl.ds(pl.multiple_of(target * part, part), part)
        return pltpu.make_async_remote_copy(
            src_ref=gates.at[rows, cols],
            dst_ref=all_g.at[mine, rows],
            send_sem=gs_sem.at[k - 1],
            recv_sem=gr_sem.at[k - 1],
            device_id=(base + target,),
            device_id_type=MESH,
        )

    def rows_of(step):
        return pl.ds(pl.multiple_of(step * envs, envs), envs)

    every = pl.ds(0, steps * envs)

    for k in range(1, group):
        x_copy(k).start()

    x_b = x_ref[...].astype(bf16)
    for n in range(0, 4 * hidden, 512):
        gates[:, n : n + 512] = (
            jnp.dot(x_b, w_ref[:width_in, n : n + 512], preferred_element_type=f32)
            + bias_ref[:, n : n + 512]
        )
    h_now[...] = h0_ref[...].astype(f32)
    c_now[...] = c0_ref[...]

    def advance(step, carry):
        rows = rows_of(step)

        @pl.when(step > 0)
        def _():
            for k in range(1, chips):
                h_copy(k, rows_of(step - 1)).start()

        keep = reset_ref[...] != step
        h_kept = jnp.where(keep, h_now[...], 0.0)
        all_h[mine, rows, :] = h_kept
        hk_b[...] = h_kept.astype(bf16)
        for n in range(0, hidden, chunk):
            pre = []
            for gate in range(4):
                cols = slice(gate * hidden + n, gate * hidden + n + chunk)
                pre.append(
                    gates[rows, cols]
                    + jnp.dot(hk_b[...], w_ref[width_in:, cols], preferred_element_type=f32)
                )
            gi, gf, gc, go = (sigmoid(pre[0]), sigmoid(pre[1]), jnp.tanh(pre[2]), sigmoid(pre[3]))
            c_kept = jnp.where(keep, c_now[:, n : n + chunk], 0.0)
            c_new = gf * c_kept + gi * gc
            tc = jnp.tanh(c_new)
            h_new = (go * tc).astype(bf16)
            for gate, value in enumerate((gi, gf, gc, go)):
                gates[rows, gate * hidden + n : gate * hidden + n + chunk] = value
            ck_all[rows, n : n + chunk] = c_kept
            tc_all[rows, n : n + chunk] = tc
            c_now[:, n : n + chunk] = c_new
            h_now[:, n : n + chunk] = h_new.astype(f32)
            hseq[rows, n : n + chunk] = h_new
        return carry

    lax.fori_loop(0, steps, advance, 0)
    for k in range(1, chips):
        h_copy(k, rows_of(steps - 1)).start()

    logits = jnp.dot(hseq[...], hw_ref[...], preferred_element_type=f32)
    col = lax.broadcasted_iota(jnp.int32, logits.shape, 1)
    is_policy = col < policy_cols
    policy = jnp.where(is_policy, logits, 0.0)
    exp_policy = jnp.where(is_policy, jnp.exp(policy), 0.0)
    sum_exp = jnp.dot(
        exp_policy, same_ref[...], preferred_element_type=f32, precision=lax.Precision.HIGHEST
    )
    sum_exp = jnp.where(is_policy, sum_exp, 1.0)
    probs = exp_policy / sum_exp
    log_probs = policy - jnp.log(sum_exp)
    taken = jnp.dot(act_ref[...], spread_ref[...], preferred_element_type=f32)
    hit = (taken == level_ref[...]) & is_policy
    token_logp = jnp.sum(jnp.where(hit, log_probs, 0.0), axis=1, keepdims=True)
    log_ratio = token_logp - aux_ref[:, 0:1]
    ratio = jnp.exp(log_ratio)
    kl_ref[...] = jnp.sum(ratio - 1.0 - log_ratio, axis=0, keepdims=True)
    grad_logp = kl_coef * (ratio - 1.0) - aux_ref[:, 1:2] * ratio
    grad_policy = grad_logp * (jnp.where(hit, 1.0, 0.0) - probs)
    grad_value = value_coef * (logits - aux_ref[:, 2:3])
    grad_logits = jnp.where(
        is_policy, grad_policy, jnp.where(col == policy_cols, grad_value, 0.0)
    ).astype(bf16)
    dh_ref[...] = lax.dot_general(hseq[...], grad_logits, TN, preferred_element_type=f32)
    head_part[...] = lax.dot_general(grad_logits, hw_ref[...], NT, preferred_element_type=f32)

    for k in range(1, chips):
        h_copy(k, every).wait_recv()
    for k in range(chips):
        forward_copy(k).start()

    h_now[...] = jnp.zeros_like(h_now)
    c_now[...] = jnp.zeros_like(c_now)

    def retreat(turn, carry):
        step = steps - 1 - turn
        rows = rows_of(step)

        @pl.when(turn > 0)
        def _():
            for k in range(1, group):
                g_copy(k, rows_of(step + 1)).start()

        keep = reset_ref[...] != step
        for n in range(0, hidden, chunk):
            here = slice(n, n + chunk)
            gi, gf, gc, go = (
                gates[rows, gate * hidden + n : gate * hidden + n + chunk] for gate in range(4)
            )
            tc = tc_all[rows, here]
            grad_h = head_part[rows, here] + h_now[:, here]
            grad_c = c_now[:, here] + grad_h * go * (1.0 - tc * tc)
            grads = (
                grad_c * gc * (gi * (1.0 - gi)),
                grad_c * ck_all[rows, here] * (gf * (1.0 - gf)),
                grad_c * gi * (1.0 - gc * gc),
                grad_h * tc * (go * (1.0 - go)),
            )
            for gate, value in enumerate(grads):
                rounded = value.astype(bf16)
                cols = slice(gate * hidden + n, gate * hidden + n + chunk)
                gg_b[:, cols] = rounded
                gates[rows, cols] = rounded.astype(f32)
            c_now[:, here] = jnp.where(keep, grad_c * gf, 0.0)
        for n in range(0, hidden, chunk):
            back = lax.dot_general(
                gg_b[...],
                w_ref[width_in + n : width_in + n + chunk, :],
                NT,
                preferred_element_type=f32,
            )
            h_now[:, n : n + chunk] = jnp.where(keep, back, 0.0)
        return carry

    lax.fori_loop(0, steps, retreat, 0)
    for k in range(1, group):
        g_copy(k, rows_of(0)).start()

    all_x[mine] = x_ref[...]
    all_g[mine] = gates[:, pl.ds(pl.multiple_of(mine * part, part), part)]
    db_ref[...] = jnp.sum(gates[...], axis=0, keepdims=True)

    for k in range(1, group):
        x_copy(k).wait()
    for k in range(1, chips):
        h_copy(k, every).wait_send()
    for k in range(chips):
        forward_copy(k).wait()
    for k in range(1, group):
        source = lax.rem(mine + k, group)
        cols = pl.ds(pl.multiple_of(source * part, part), part)
        g_copy(k, every).wait()

    dw_ref[...] = jnp.zeros_like(dw_ref)

    def gather(source, carry):
        g_b = all_g[source].astype(bf16)
        x_part = lax.dot_general(all_x[source].astype(bf16), g_b, TN, preferred_element_type=f32)
        dw_ref[:width_in, :] += x_part
        for n in range(0, hidden, chunk):
            h_b = all_h[source, :, n : n + chunk].astype(bf16)
            dw_ref[width_in + n : width_in + n + chunk, :] += lax.dot_general(
                h_b, g_b, TN, preferred_element_type=f32
            )
        return carry

    lax.fori_loop(0, group, gather, 0)


def shards(
    observations,
    physics_params,
    actions,
    reset_step,
    hidden_start,
    cell_start,
    old_logp,
    advantages,
    returns,
    lstm_weight,
    lstm_bias,
    head_weight,
):
    devices = lax.axis_size("env")
    group = math.gcd(devices, 8)
    slabs = devices // group
    steps, envs, obs = observations.shape
    hidden = hidden_start.shape[1]
    total_in, gate_cols = lstm_weight.shape
    width_in = total_in - hidden
    act_count = actions.shape[2]
    head_cols = head_weight.shape[1]
    policy_cols = head_cols - 1
    bins = policy_cols // act_count
    lanes = -(-head_cols // 128) * 128
    tokens = steps * envs
    token_total = tokens * devices
    part = gate_cols // group

    adv_sums = lax.psum(jnp.stack([jnp.sum(advantages), jnp.sum(advantages * advantages)]), "env")
    adv_mean = adv_sums[0] / token_total
    spread = adv_sums[1] / token_total - adv_mean * adv_mean
    norm_adv = (advantages - adv_mean) / jnp.sqrt(spread + spread_floor)
    aux = jnp.stack([old_logp.reshape(-1), norm_adv.reshape(-1), returns.reshape(-1)], axis=1)

    phys = jnp.broadcast_to(physics_params[None], (steps, envs, physics_params.shape[1]))
    x = jnp.concatenate([observations, phys], axis=2).reshape(tokens, width_in).astype(f32)
    act = jnp.pad(actions.reshape(tokens, act_count), ((0, 0), (0, 128 - act_count))).astype(bf16)
    head_wide = jnp.pad(head_weight, ((0, 0), (0, lanes - head_cols)))
    col = jnp.arange(lanes)
    joint = jnp.where(col < policy_cols, col // bins, -1)
    same = ((joint[:, None] == joint[None, :]) & (joint[:, None] >= 0)).astype(f32)
    spread_map = (jnp.arange(128)[:, None] == joint[None, :]).astype(bf16)
    level = (col % bins).astype(f32)[None, :]

    vmem = pl.BlockSpec(memory_space=pltpu.VMEM)
    dma = pltpu.SemaphoreType.DMA
    chips = group // 2
    dw, db, dh, kl = pl.pallas_call(
        functools.partial(kernel, (steps, envs, hidden, width_in, group, policy_cols)),
        out_shape=(
            jax.ShapeDtypeStruct((total_in, part), f32),
            jax.ShapeDtypeStruct((1, gate_cols), f32),
            jax.ShapeDtypeStruct((hidden, lanes), f32),
            jax.ShapeDtypeStruct((1, 1), f32),
        ),
        in_specs=[vmem] * 12,
        out_specs=(vmem,) * 4,
        scratch_shapes=[
            pltpu.VMEM((tokens, gate_cols), f32),
            pltpu.VMEM((tokens, hidden), f32),
            pltpu.VMEM((tokens, hidden), f32),
            pltpu.VMEM((tokens, hidden), bf16),
            pltpu.VMEM((envs, hidden), bf16),
            pltpu.VMEM((envs, hidden), f32),
            pltpu.VMEM((envs, hidden), f32),
            pltpu.VMEM((envs, gate_cols), bf16),
            pltpu.VMEM((tokens, hidden), f32),
            pltpu.VMEM((group, tokens, hidden), f32),
            pltpu.VMEM((group, tokens, part), f32),
            pltpu.VMEM((group, tokens, width_in), f32),
            dma((chips - 1,)),
            dma((chips - 1,)),
            dma((chips,)),
            dma((chips,)),
            dma((group - 1,)),
            dma((group - 1,)),
            dma((group - 1,)),
            dma((group - 1,)),
        ],
        compiler_params=pltpu.CompilerParams(
            collective_id=0, has_side_effects=True, vmem_limit_bytes=60 * 1024 * 1024
        ),
    )(
        x,
        act,
        reset_step[:, None],
        hidden_start,
        cell_start,
        aux,
        lstm_weight,
        lstm_bias[None, :],
        head_wide,
        same,
        spread_map,
        level,
    )

    small = jnp.concatenate(
        [dh[:, :head_cols].reshape(devices, -1), db.reshape(devices, -1)], axis=1
    )
    small_part = lax.psum_scatter(small, "env", scatter_dimension=0, tiled=True)[0]
    head_rows = hidden // devices
    head_part = small_part[: head_rows * head_cols].reshape(head_rows, head_cols)
    bias_part = small_part[head_rows * head_cols :]

    along = [[slab * group + j for slab in range(slabs)] for j in range(group)]
    inside = [[slab * group + j for j in range(group)] for slab in range(slabs)]
    slab_rows = total_in // slabs
    own_rows = total_in // devices
    dw = lax.psum_scatter(
        dw.reshape(slabs, slab_rows, part),
        "env",
        scatter_dimension=0,
        axis_index_groups=along,
        tiled=True,
    )
    dw = lax.all_to_all(
        dw.reshape(group, own_rows, part), "env", 0, 0, axis_index_groups=inside, tiled=True
    )
    lstm_part = dw.transpose(1, 0, 2).reshape(own_rows, gate_cols)
    local_squares = jnp.sum(dw * dw) + jnp.sum(small_part * small_part)
    totals = lax.psum(jnp.stack([local_squares, kl[0, 0]]), "env")
    param_total = lstm_weight.size + lstm_bias.size + head_weight.size
    scale = 1.0 / jnp.sqrt(totals[0] / param_total + 1.0)
    return (lstm_part * scale, bias_part * scale, head_part * scale, totals[1] / token_total)


def solution(mesh):
    in_specs = (
        P(None, "env", None),
        P("env", None),
        P(None, "env", None),
        P("env"),
        P("env", None),
        P("env", None),
        P(None, "env"),
        P(None, "env"),
        P(None, "env"),
        P(),
        P(),
        P(),
    )
    out_specs = (P("env", None), P("env"), P("env", None), P())
    return jax.shard_map(shards, mesh=mesh, in_specs=in_specs, out_specs=out_specs, check_vma=False)
```

time: 764 us -> 437 us (0.57)
  blocking collectives: 358 us -> 82.5 us
  matrix products: 191 us -> 0 us
  waiting for transfers between devices: 0.05 us -> 178 us
  Pallas kernels: 0 us -> 120 us
  other arithmetic: 101 us -> 15.1 us
  local copies, waits for them, and re-layouts: 62.8 us -> 14.5 us
  starting transfers between devices: 24.3 us -> 3.74 us
    unnamed x2 -> x0, blocking collectives: 275 us -> none
    dot_general x37 -> x0, matrix products: 191 us -> none  [the longest x16 90.5 us: retreat(): lax.dot_general(grad_gates, w_rec, (((1,), (1,)), ((), ())), preferred_el...]
    unnamed x5 -> x3, waiting for transfers between devices: 0.03 us -> 132 us
    pallas_call x0 -> x1, Pallas kernels: none -> 120 us  [shards(): pl.pallas_call(functools.partial(kernel, (steps, envs, hidden, width_in,...]
    reduce_scatter x1, waiting for transfers between devices: 0.02 us -> 45.5 us  [shards(): lax.psum_scatter(dw.reshape(slabs, slab_rows, part), 'env', scatter_dimen...]
    ne x32 -> x0, other arithmetic: 31.3 us -> none  [the longest x16 20.9 us: retreat(): keep_mask = (reset_step != step_index)[:, None]]
    dynamic_update_slice x48 -> x0, other arithmetic: 29.2 us -> none  [the longest x16 16.5 us: local_terms(): lax.scan(retreat, (zero_state, zero_state), (c_kept_all, activated_all, t...]
    dynamic_slice x32 -> x0, local copies, waits for them, and re-layouts: 29.2 us -> none  [local_terms(): lax.scan(advance, (hidden_start, cell_start), (projected, step_ids))]
  transfers between devices with their start and end apart: 5 -> 3, of which waited for: 0 -> 2; matrix products, arithmetic and copies ran while one was open for 57% -> 1% of each run, Pallas kernels for 0% -> 0%
where the time goes in v1:
time: 437 us; the launch traced here: 435 us
  waiting for transfers between devices  178 us (41%)
  Pallas kernels  120 us (27%)
  blocking collectives  82.5 us (19%)
  between operations  22 us (5%)
  other arithmetic  15.1 us (3%)
  local copies, waits for them, and re-layouts  14.5 us (3%)
    unnamed x3, waiting for transfers between devices  132 us
    pallas_call x1, Pallas kernels, shards(): pl.pallas_call(functools.partial(kernel, (steps, envs, hidden, width_in,...  120 us
    reduce_scatter x1, waiting for transfers between devices, shards(): lax.psum_scatter(dw.reshape(slabs, slab_rows, part), 'env', scatter_dimen...  45.5 us
    psum x1, blocking collectives, shards(): lax.psum(jnp.stack([jnp.sum(advantages), jnp.sum(advantages * advantages)...  42 us
    psum x1, blocking collectives, shards(): totals = lax.psum(jnp.stack([local_squares, kl[0, 0]]), 'env')  40.5 us
  transfers between devices with their start and end apart: 3, of which 2 were waited for; matrix products, arithmetic and copies ran while one was open for 1% of the time, Pallas kernels for 0%

profile of v1, /device:TPU:0, one launch (start us, length us, event | category | flops | bytes accessed | tf_op | source)
XLA Modules:
  0.0 435.5 jit_solution(1194394533574343379)
XLA Ops:
  8.6 1.3 fusion.6
  10.0 1.4 pad_maximum_fusion.3
  11.3 42.0 %psum.14 = f32[2]{0:T(128)S(1)} all-reduce(f32[2]{0:T(128)S(1)} %pad_maximum_fusion.3), channel_id=1, replica_groups=mesh['env'=32] {'env'}, use_global_device_ids=true, to_apply=%region_2.0 | all-reduce | flops 2 | bytes 16 | tf_op jit(solution)/shard_map/psum | solution.py:323
  56.6 0.7 subtract_divide_fusion
  57.3 0.8 stack_reshape.11
  58.1 0.8 stack_reshape.9
  58.9 0.8 copy.32.aux_ref
  59.7 0.6 fusion.spread_ref
  60.3 0.8 and_convert_fusion.same_ref
  61.2 1.2 copy.30
  62.4 0.7 broadcast_in_dim.8
  63.1 0.9 pad_maximum_fusion.1
  64.0 0.7 bitcast_convert_fusion.x_ref
  64.7 0.9 convert.6
  65.6 0.9 pad.10.hw_ref
  66.5 0.6 pad.9.act_ref
  67.1 1.3 copy.31.reset_ref
  68.5 119.8 %shard_map.147 = (f32[1152,512]{1,0:T(8,128)}, f32[1,4096]{1,0:T(1,128)}, f32[1024,256]{1,0:T(8,128)}, f32[1,1]{1,0:T(1,128)}) custom-call(f32[256,128]{1,0:T(8,128)} %bitcast_convert_fusion.x_ref, bf16[256,128]{1,0:T(8,128)(2,1)} %pad.9.act_ref, s32[16,1]{1,0:T(8,128)} %copy.31.reset_ref, bf16[16,1024]{1,0:T(8,128)(2,1)} %h0_ref.1, f32[16,1024]{1,0:T(8,128)} %c0_ref.1, ...), custom_call_target="tpu_custom_call" | custom-call | tf_op jit(solution)/shard_map/pallas_call | solution.py:342
  188.2 1.8 reshape.118
  190.0 45.5 %reduce-scatter.2.cloned.1.call-done = f32[1,288,512]{2,1,0:T(8,128)} async-done(((f32[4,288,512]{2,1,0:T(8,128)}), f32[1,288,512]{2,1,0:T(8,128)}) %reduce-scatter.2.cloned.1.call-update) | async-done | bytes 589840 | tf_op jit(solution)/shard_map/reduce_scatter | solution.py:404
  235.6 2.0 reshape.117
  237.5 3.7 all-to-all-start
  241.2 1.8 pad_maximum_fusion
  243.0 132.4 %all-reduce.5.cloned.1.call-done = f32[32,7200]{1,0:T(8,128)} async-done(((f32[32,7200]{1,0:T(8,128)}), f32[32,7200]{1,0:T(8,128)}) %all-reduce.5.cloned.1.call-update) | async-done | bytes 921616
  375.4 1.6 fusion.1
  377.0 0.8 multiply_reduce_fusion
  379.1 0.6 pad_maximum_fusion.4
  379.7 40.5 %psum.15 = f32[2]{0:T(128)S(1)} all-reduce(f32[2]{0:T(128)S(1)} %pad_maximum_fusion.4), channel_id=1, replica_groups=mesh['env'=32] {'env'}, use_global_device_ids=true, to_apply=%region_7.8 | all-reduce | flops 2 | bytes 16 | tf_op jit(solution)/shard_map/psum | solution.py:416
  421.5 1.0 fusion.2
  422.5 0.7 mul.60
  423.7 1.2 copy.34
  425.6 1.3 fusion.5
  (15 shorter events, 2.4 us)
Async XLA Ops:
  8.0 227.6 %reduce-scatter.2.cloned.1.call-start = ((), (), s32[]{:S(2)}) async-start(), calls=%async_computation.2 | async-start | bytes 2949120 | tf_op jit(solution)/shard_map/reduce_scatter | solution.py:404
  237.5 139.5 %all-to-all-start = ((f32[8,36,512]{2,1,0:T(8,128)}), f32[8,36,512]{2,1,0:T(8,128)S(1)}, u32[]{:S(2)}, u32[]{:S(2)}) async-start(f32[8,36,512]{2,1,0:T(8,128)} %reshape.117), calls=%async_computation.1 | async-start | bytes 1310720 | tf_op jit(solution)/shard_map/all_to_all | solution.py:411
  241.2 134.2 %all-reduce.5.cloned.1.call-start = ((), (), s32[]{:S(2)}) async-start(), calls=%async_computation.3 | async-start | bytes 1867776
Sparse Core Ops, SparseCore 0:
  188.4 47.1 reduce-scatter.1
Sparse Core Ops, SparseCore 1:
  246.9 128.5 all-reduce.4
